TPU v7x, 128 devices: a whole 4x4x4 slice. The times are simulated.
128 devices in a mesh: fsdp: 8 (over x, y_lo), tensor: 16 (over z, y_hi, core).
Axes of the slice: x: 4, y: 4 (y_hi: 2, y_lo: 2; y = y_hi * 2 + y_lo), z: 4, core: 2. Of those that a mesh axis runs over, the one named last changes fastest.
Arguments:
- modality: int32 [8192], P('fsdp'), may hold values from 0 to 2, as said below
- out_grad: bfloat16 [8192, 4096], P('fsdp', 'tensor'), may hold values from -6 to 6
- gate_pre: bfloat16 [8192, 11008], P('fsdp', 'tensor'), may hold values from -6 to 6
- up_pre: bfloat16 [8192, 11008], P('fsdp', 'tensor'), may hold values from -6 to 6
- down_weight: bfloat16 [3, 11008, 4096], P(None, 'tensor', 'fsdp'), may hold values from -0.0546875 to 0.0546875
Outputs:
- down_grad: float32 [3, 11008, 4096], P(None, 'tensor', 'fsdp')
- gate_grad: bfloat16 [8192, 11008], P('fsdp', 'tensor')
- up_grad: bfloat16 [8192, 11008], P('fsdp', 'tensor')
Inputs may be any that keep to these rules, and one draw needn't show every extreme that they name: `modality`: the 1024 tokens of every index of fsdp hold each of the three modalities at least once.
All inputs are finite; a program needn't handle non-finite values.
Results may differ from a plain program's by a relative error of at most 0.012.
Values may be sent and summed in bfloat16 or wider, within the bound.
No kernel may reach another device: no remote copies, remote signals or barrier semaphores. Data moves between devices by JAX's collectives and lax.ppermute only.
A program may use at most 256 MiB of HBM per device.

v0:
```python
import math
import jax
import jax.numpy as jnp
from jax import lax
from jax.sharding import Mesh
from jax.sharding import PartitionSpec as P

FSDP = ("fsdp_0", "fsdp_1")


def sent_to_all(shard, axis):
    peers = lax.axis_size(axis)
    return lax.all_to_all(
        jnp.broadcast_to(shard[None], (peers, *shard.shape)), axis, 0, 0, tiled=True
    )


def taken_together(shard, axis):
    return sent_to_all(shard, axis).sum(axis=0)


def gather_axes(shard, axes, dim):
    for axis in reversed(axes):
        shard = lax.all_gather(shard, axis, axis=dim, tiled=True)
    return shard


def sum_by_axis(shard, axes, dim):
    for axis in axes:
        shard = lax.psum_scatter(shard, axis, scatter_dimension=dim, tiled=True)
    return shard


def kind_table(kind_ids):
    labels = jnp.arange(3, dtype=jnp.int32)
    return (kind_ids[:, None] == labels[None, :]).astype(jnp.float32)


def shards(modality, out_grad, gate_pre, up_pre, down_weight):
    tok_rows = modality.shape[0]
    groups = lax.axis_size(FSDP)
    local_onehot = kind_table(modality)
    counts = taken_together(jnp.sum(local_onehot, axis=0), FSDP)
    factor = tok_rows * groups / (3.0 * counts)
    token_scale = jnp.sum(local_onehot * factor[None, :], axis=1)
    scaled_part = (out_grad.astype(jnp.float32) * token_scale[:, None]).astype(jnp.bfloat16)
    scaled = lax.all_gather(scaled_part, "tensor", axis=1, tiled=True)
    gate_val = gate_pre.astype(jnp.float32)
    up_val = up_pre.astype(jnp.float32)
    sigmoid_g = jax.nn.sigmoid(gate_val)
    active = gate_val * sigmoid_g
    hidden = (active * up_val).astype(jnp.bfloat16)
    hid_cols = hidden.shape[1]
    width_all = scaled.shape[1]
    block_rows = math.gcd(tok_rows, 128)
    block_count = tok_rows // block_rows + 2
    capacity = block_count * block_rows
    int_onehot = local_onehot.astype(jnp.int32)
    slot_rank = jnp.sum((jnp.cumsum(int_onehot, axis=0) - int_onehot) * int_onehot, axis=1)
    used_rows = jnp.sum(int_onehot, axis=0)
    padded = (used_rows + block_rows - 1) // block_rows * block_rows
    second = padded[0]
    third_start = padded[0] + padded[1]
    starts = jnp.stack([jnp.zeros((), jnp.int32), second, third_start])
    slot_index = jnp.sum(int_onehot * starts[None, :], axis=1) + slot_rank
    block_first = jnp.arange(block_count, dtype=jnp.int32) * block_rows
    block_kind = (block_first >= second).astype(jnp.int32) + (block_first >= third_start).astype(
        jnp.int32
    )
    packed_scaled = jnp.zeros((capacity, width_all), jnp.bfloat16).at[slot_index].set(scaled)
    packed_hidden = jnp.zeros((capacity, hid_cols), jnp.bfloat16).at[slot_index].set(hidden)
    weight_piece = gather_axes(down_weight, FSDP, 2)
    columns_here = weight_piece.shape[2]
    columns = packed_scaled
    columns = columns.reshape(block_count, block_rows, columns_here)
    chosen = jnp.take(weight_piece, block_kind, axis=0)
    product = jnp.einsum("bkw,bfw->bkf", columns, chosen, preferred_element_type=jnp.float32)
    folded = product.reshape(capacity, hid_cols)
    d_hidden = folded[slot_index]
    up_grad = (d_hidden * active).astype(jnp.bfloat16)
    slope = sigmoid_g * (1.0 + gate_val * (1.0 - sigmoid_g))
    gate_grad = (d_hidden * up_val * slope).astype(jnp.bfloat16)

    def kind_product(kind_id):
        first_block = starts[kind_id] // block_rows
        last_block = first_block + padded[kind_id] // block_rows

        def add_block(block_index, running):
            rows_hidden = lax.dynamic_slice_in_dim(
                packed_hidden, block_index * block_rows, block_rows, 0
            )
            rows_scaled = lax.dynamic_slice_in_dim(
                packed_scaled, block_index * block_rows, block_rows, 0
            )
            return running + lax.dot_general(
                rows_hidden,
                rows_scaled,
                (((0,), (0,)), ((), ())),
                preferred_element_type=jnp.float32,
            )

        return lax.fori_loop(
            first_block, last_block, add_block, jnp.zeros((hid_cols, width_all), jnp.float32)
        )

    partial_sum = jnp.stack([kind_product(kind_id) for kind_id in range(3)])
    down_grad = sum_by_axis(partial_sum.astype(jnp.bfloat16), FSDP, 2).astype(jnp.float32)
    return (down_grad, gate_grad, up_grad)


def solution(mesh):
    torus = Mesh(mesh.devices.reshape(4, 2, mesh.shape["tensor"]), ("fsdp_0", "fsdp_1", "tensor"))
    in_specs = (
        P(FSDP),
        P(FSDP, "tensor"),
        P(FSDP, "tensor"),
        P(FSDP, "tensor"),
        P(None, "tensor", FSDP),
    )
    out_specs = (P(None, "tensor", FSDP), P(FSDP, "tensor"), P(FSDP, "tensor"))
    return jax.shard_map(
        shards, mesh=torus, in_specs=in_specs, out_specs=out_specs, check_vma=False
    )
```

profile of v0, /device:TPU:1, one launch (start us, length us, event | category | flops | bytes accessed | tf_op | source)
XLA Modules:
  0.0 537.5 jit_solution(230502349124138979)
XLA Ops:
  7.2 0.0 all-gather.6.cloned.1.call-start
  7.2 0.7 all-gather.6.cloned.1.call-update
  7.9 0.8 convert_reduce_fusion
  8.7 0.6 broadcast_in_dim.15
  9.3 5.9 %all-to-all-start = ((f32[8,1,3]{2,1,0:T(1,128)}), f32[8,1,3]{2,1,0:T(1,128)S(1)}, u32[]{:S(2)}, u32[]{:S(2)}) async-start(f32[8,1,3]{2,1,0:T(1,128)} %broadcast_in_dim.15), calls=%async_computation | async-start | bytes 8192 | tf_op jit(solution)/shard_map/all_to_all | solution.py:13
  15.2 0.0 all-gather.4.cloned.1.call-start
  15.2 4.9 all-to-all-done
  20.2 0.8 select_reduce_fusion
  20.9 2.1 multiply_convert_fusion.1
  23.1 0.0 all-gather.4.cloned.1.call-update
  23.1 0.0 all-gather.8.cloned.1.call-start
  23.1 49.2 %all-gather.6.cloned.1.call-done = bf16[3,688,1024]{2,1,0:T(8,128)(2,1)} async-done(((bf16[3,688,512]{2,1,0:T(8,128)(2,1)}), bf16[3,688,1024]{2,1,0:T(8,128)(2,1)}) %all-gather.6.cloned.1.call-update) | async-done | bytes 4227088 | tf_op jit(solution)/shard_map/all_gather | solution.py:24
  72.3 0.0 all-gather.8.cloned.1.call-update
  72.4 0.0 reduce-scatter.3.cloned.1.call-start
  72.4 0.1 fusion.30
  72.5 0.7 fusion.40
  82.2 0.9 reduce-window.6
  83.0 0.2 slice_reduce_fusion
  83.3 0.2 reduce-window.9
  83.4 0.7 copy.28
  84.2 2.2 copy.29
  86.4 0.7 pad_add_fusion
  87.2 0.1 add_bitcast_fusion
  87.2 0.1 fusion.32
  87.4 7.4 %scatter_custom_fusion = bf16[1280,688]{1,0:T(8,128)(2,1)} fusion(s32[1024]{0:T(1024)S(1)} %bitcast.34, bf16[1024,688]{1,0:T(8,128)(2,1)S(1)} %copy.29, bf16[1024,688]{1,0:T(8,128)(2,1)S(1)} %copy.28, f32[]{:T(128)} %constant.119.clone.1, bf16[]{:T(256)} %constant.116.clone.1), kind=kCustom, calls=%fused_computation.46 | custom fusion | flops 5636096 | bytes 4907014 | tf_op jit(solution)/shard_map/scatter | solution.py:71
  94.8 58.6 %all-gather.4.cloned.1.call-done = bf16[1024,4096]{1,0:T(8,128)(2,1)} async-done(((bf16[1024,256]{1,0:T(8,128)(2,1)}), bf16[1024,4096]{1,0:T(8,128)(2,1)}) %all-gather.4.cloned.1.call-update) | async-done | bytes 8388624 | tf_op jit(solution)/shard_map/all_gather | solution.py:47
  153.4 19.3 %scatter_custom_fusion.1 = bf16[1280,4096]{1,0:T(8,128)(2,1)} fusion(s32[1024]{0:T(1024)S(1)} %bitcast.35, bf16[1024,4096]{1,0:T(8,128)(2,1)} %all-gather.4.cloned.1.call-done, bf16[]{:T(256)} %constant.116.clone.1), kind=kCustom, calls=%fused_computation.30 | custom fusion | bytes 10486272 | tf_op jit(solution)/shard_map/scatter | solution.py:70
  172.7 5.6 %broadcast.148.clone.2 = f32[688,4096]{1,0:T(8,128)} broadcast(f32[]{:T(128)} %constant.110.clone.1), dimensions={} | broadcast | bytes 11272196 | tf_op jit(solution)/shard_map/broadcast.21
  178.4 31.6 %while.30 = (s32[]{:T(128)}, f32[688,4096]{1,0:T(8,128)}, s32[]{:T(128)}, bf16[1280,688]{1,0:T(8,128)(2,1)}, bf16[1280,4096]{1,0:T(8,128)(2,1)}, /*index=5*/s32[]{:T(128)}, s32[]{:T(128)}, s32[]{:T(128)}, s32[]{:T(128)}) while((s32[]{:T(128)}, f32[688,4096]{1,0:T(8,128)}, s32[]{:T(128)}, bf16[1280,688]{1,0:T(8,128)(2,1)}, ...), condition=%wide.region_11.12_spmd, body=%wide.region_10.11_spmd.sunk | while | flops 724238336 | bytes 23790732 | solution.py:102
  178.4 10.5 %convolution_add_fusion.6 = f32[688,4096]{1,0:T(8,128)} fusion(f32[688,4096]{1,0:T(8,128)} %get-tuple-element.306, bf16[1280,4096]{1,0:T(8,128)(2,1)} %get-tuple-element.318, s32[]{:T(128)S(6)} %select_n.91, bf16[1280,688]{1,0:T(8,128)(2,1)} %get-tuple-element.317), kind=kOutput, calls=%fused_computation.6.clone.1 | convolution fusion | flops 724238336 | bytes 23790592 | tf_op jit(solution)/shard_map/while/body/dot_general | solution.py:95
  188.9 10.5 %convolution_add_fusion.6 = f32[688,4096]{1,0:T(8,128)} fusion(f32[688,4096]{1,0:T(8,128)} %get-tuple-element.306, bf16[1280,4096]{1,0:T(8,128)(2,1)} %get-tuple-element.318, s32[]{:T(128)S(6)} %select_n.91, bf16[1280,688]{1,0:T(8,128)(2,1)} %get-tuple-element.317), kind=kOutput, calls=%fused_computation.6.clone.1 | convolution fusion | flops 724238336 | bytes 23790592 | tf_op jit(solution)/shard_map/while/body/dot_general | solution.py:95
  199.4 10.6 %convolution_add_fusion.6 = f32[688,4096]{1,0:T(8,128)} fusion(f32[688,4096]{1,0:T(8,128)} %get-tuple-element.306, bf16[1280,4096]{1,0:T(8,128)(2,1)} %get-tuple-element.318, s32[]{:T(128)S(6)} %select_n.91, bf16[1280,688]{1,0:T(8,128)(2,1)} %get-tuple-element.317), kind=kOutput, calls=%fused_computation.6.clone.1 | convolution fusion | flops 724238336 | bytes 23790592 | tf_op jit(solution)/shard_map/while/body/dot_general | solution.py:95
  210.0 7.7 %convert_bitcast_fusion.2 = bf16[1,688,4096]{2,1,0:T(8,128)(2,1)} fusion(f32[688,4096]{1,0:T(8,128)} %get-tuple-element.87), kind=kLoop, calls=%fused_computation.29 | loop fusion | flops 2818048 | bytes 16908288 | tf_op jit(solution)/shard_map/stack | solution.py:106
  217.7 5.5 %broadcast.148.clone.1 = f32[688,4096]{1,0:T(8,128)} broadcast(f32[]{:T(128)} %constant.110.clone.1), dimensions={} | broadcast | bytes 11272196 | tf_op jit(solution)/shard_map/broadcast.21
  223.2 20.8 %while.31 = (s32[]{:T(128)}, f32[688,4096]{1,0:T(8,128)}, s32[]{:T(128)}, bf16[1280,688]{1,0:T(8,128)(2,1)}, bf16[1280,4096]{1,0:T(8,128)(2,1)}, /*index=5*/s32[]{:T(128)}, s32[]{:T(128)}, s32[]{:T(128)}, s32[]{:T(128)}) while((s32[]{:T(128)}, f32[688,4096]{1,0:T(8,128)}, s32[]{:T(128)}, bf16[1280,688]{1,0:T(8,128)(2,1)}, ...), condition=%wide.region_13.14_spmd, body=%wide.region_12.13_spmd.sunk | while | flops 724238336 | bytes 23790732 | solution.py:102
  223.2 10.4 %convolution_add_fusion.7 = f32[688,4096]{1,0:T(8,128)} fusion(f32[688,4096]{1,0:T(8,128)} %get-tuple-element.279, bf16[1280,4096]{1,0:T(8,128)(2,1)} %get-tuple-element.291, s32[]{:T(128)S(6)} %select_n.92, bf16[1280,688]{1,0:T(8,128)(2,1)} %get-tuple-element.290), kind=kOutput, calls=%fused_computation.10.clone.1 | convolution fusion | flops 724238336 | bytes 23790592 | tf_op jit(solution)/shard_map/while/body/dot_general | solution.py:95
  233.6 10.4 %convolution_add_fusion.7 = f32[688,4096]{1,0:T(8,128)} fusion(f32[688,4096]{1,0:T(8,128)} %get-tuple-element.279, bf16[1280,4096]{1,0:T(8,128)(2,1)} %get-tuple-element.291, s32[]{:T(128)S(6)} %select_n.92, bf16[1280,688]{1,0:T(8,128)(2,1)} %get-tuple-element.290), kind=kOutput, calls=%fused_computation.10.clone.1 | convolution fusion | flops 724238336 | bytes 23790592 | tf_op jit(solution)/shard_map/while/body/dot_general | solution.py:95
  244.0 5.6 %broadcast.148.clone = f32[688,4096]{1,0:T(8,128)} broadcast(f32[]{:T(128)} %constant.110.clone.1), dimensions={} | broadcast | bytes 11272196 | tf_op jit(solution)/shard_map/broadcast.21
  249.6 42.1 %while.32 = (s32[]{:T(128)}, f32[688,4096]{1,0:T(8,128)}, s32[]{:T(128)}, bf16[1280,688]{1,0:T(8,128)(2,1)}, bf16[1280,4096]{1,0:T(8,128)(2,1)}, /*index=5*/s32[]{:T(128)}, s32[]{:T(128)}, s32[]{:T(128)}, s32[]{:T(128)}) while((s32[]{:T(128)}, f32[688,4096]{1,0:T(8,128)}, s32[]{:T(128)}, bf16[1280,688]{1,0:T(8,128)(2,1)}, ...), condition=%wide.region_15.16_spmd, body=%wide.region_14.15_spmd.sunk | while | flops 724238336 | bytes 23790732 | solution.py:102
  249.6 10.6 %convolution_add_fusion.8 = f32[688,4096]{1,0:T(8,128)} fusion(f32[688,4096]{1,0:T(8,128)} %get-tuple-element.252, bf16[1280,4096]{1,0:T(8,128)(2,1)} %get-tuple-element.264, s32[]{:T(128)S(6)} %select_n.93, bf16[1280,688]{1,0:T(8,128)(2,1)} %get-tuple-element.263), kind=kOutput, calls=%fused_computation.14.clone.1 | convolution fusion | flops 724238336 | bytes 23790592 | tf_op jit(solution)/shard_map/while/body/dot_general | solution.py:95
  260.2 10.6 %convolution_add_fusion.8 = f32[688,4096]{1,0:T(8,128)} fusion(f32[688,4096]{1,0:T(8,128)} %get-tuple-element.252, bf16[1280,4096]{1,0:T(8,128)(2,1)} %get-tuple-element.264, s32[]{:T(128)S(6)} %select_n.93, bf16[1280,688]{1,0:T(8,128)(2,1)} %get-tuple-element.263), kind=kOutput, calls=%fused_computation.14.clone.1 | convolution fusion | flops 724238336 | bytes 23790592 | tf_op jit(solution)/shard_map/while/body/dot_general | solution.py:95
  270.8 10.5 %convolution_add_fusion.8 = f32[688,4096]{1,0:T(8,128)} fusion(f32[688,4096]{1,0:T(8,128)} %get-tuple-element.252, bf16[1280,4096]{1,0:T(8,128)(2,1)} %get-tuple-element.264, s32[]{:T(128)S(6)} %select_n.93, bf16[1280,688]{1,0:T(8,128)(2,1)} %get-tuple-element.263), kind=kOutput, calls=%fused_computation.14.clone.1 | convolution fusion | flops 724238336 | bytes 23790592 | tf_op jit(solution)/shard_map/while/body/dot_general | solution.py:95
  281.3 10.5 %convolution_add_fusion.8 = f32[688,4096]{1,0:T(8,128)} fusion(f32[688,4096]{1,0:T(8,128)} %get-tuple-element.252, bf16[1280,4096]{1,0:T(8,128)(2,1)} %get-tuple-element.264, s32[]{:T(128)S(6)} %select_n.93, bf16[1280,688]{1,0:T(8,128)(2,1)} %get-tuple-element.263), kind=kOutput, calls=%fused_computation.14.clone.1 | convolution fusion | flops 724238336 | bytes 23790592 | tf_op jit(solution)/shard_map/while/body/dot_general | solution.py:95
  291.8 8.3 %convert_bitcast_fusion = (bf16[1,688,4096]{2,1,0:T(8,128)(2,1)S(1)}, bf16[1,688,4096]{2,1,0:T(8,128)(2,1)S(1)}) fusion(f32[688,4096]{1,0:T(8,128)} %get-tuple-element.89, f32[688,4096]{1,0:T(8,128)} %get-tuple-element.88), kind=kLoop, calls=%fused_computation.27 | loop fusion | flops 5636096 | bytes 33816576 | tf_op jit(solution)/shard_map/stack | solution.py:106
  300.1 10.1 %pad_maximum_fusion = bf16[3,688,4096]{2,1,0:T(8,128)(2,1)} fusion(bf16[1,688,4096]{2,1,0:T(8,128)(2,1)S(1)} %get-tuple-element.144, bf16[1,688,4096]{2,1,0:T(8,128)(2,1)S(1)} %get-tuple-element.145, bf16[1,688,4096]{2,1,0:T(8,128)(2,1)} %convert_bitcast_fusion.2), kind=kLoop, calls=%fused_computation.26 | loop fusion | flops 16908288 | bytes 33816576 | tf_op jit(solution)/shard_map/stack | solution.py:106
  310.1 0.0 reduce-scatter.3.cloned.1.call-update
  310.2 0.3 reduce-scatter.5.cloned.1.call-start
  310.5 0.6 fusion.35
  311.1 0.6 compare_and_fusion
  311.8 0.6 broadcast_clamp_fusion
  312.4 9.8 %fusion.39 = (bf16[3,688,1408]{2,1,0:T(8,128)(2,1)}, bf16[3,688,1408]{2,1,0:T(8,128)(2,1)}) fusion(bf16[3,688,4096]{2,1,0:T(8,128)(2,1)} %all-gather.8.cloned.1.call-done), kind=kLoop, calls=%fused_computation.85 | loop fusion | bytes 23248896 | tf_op jit(solution)/shard_map/jit(_take)/gather | solution.py:76
  322.1 14.4 %gather_fusion.1 = bf16[10,688,1408]{2,1,0:T(8,128)(2,1)} fusion(bf16[3,688,1408]{2,1,0:T(8,128)(2,1)} %get-tuple-element.137, s32[1024]{0:T(1024)S(1)} %pad_clamp_fusion), kind=kCustom, calls=%fused_computation.1 | custom fusion | bytes 38748200 | tf_op jit(solution)/shard_map/jit(_take)/gather | solution.py:76
  336.5 14.3 %gather_fusion.2 = bf16[10,688,1408]{2,1,0:T(8,128)(2,1)} fusion(bf16[3,688,1408]{2,1,0:T(8,128)(2,1)} %get-tuple-element.138, s32[1024]{0:T(1024)S(1)} %pad_clamp_fusion), kind=kCustom, calls=%fused_computation.2 | custom fusion | bytes 38748200 | tf_op jit(solution)/shard_map/jit(_take)/gather | solution.py:76
  350.9 5.2 mini-gather-slice.5
  356.1 11.0 %gather_fusion.3 = bf16[10,688,1280]{2,1,0:T(8,128)(2,1)} fusion(bf16[3,688,1280]{2,1,0:T(8,128)(2,1)} %mini-gather-slice.5, s32[1024]{0:T(1024)S(1)} %pad_clamp_fusion), kind=kCustom, calls=%fused_computation.3 | custom fusion | bytes 35225640 | tf_op jit(solution)/shard_map/jit(_take)/gather | solution.py:76
  367.1 100.5 %reduce-scatter.3.cloned.1.call-done = bf16[3,688,1024]{2,1,0:T(8,128)(2,1)} async-done(((bf16[3,688,4096]{2,1,0:T(8,128)(2,1)}), bf16[3,688,1024]{2,1,0:T(8,128)(2,1)}) %reduce-scatter.3.cloned.1.call-update) | async-done | bytes 4227088 | tf_op jit(solution)/shard_map/reduce_scatter | solution.py:30
  467.6 0.0 reduce-scatter.5.cloned.1.call-update
  467.6 33.8 %fusion.9 = f32[10,128,688]{2,1,0:T(8,128)} fusion(bf16[10,128,4096]{2,1,0:T(8,128)(2,1)} %bitcast.31, bf16[10,688,1280]{2,1,0:T(8,128)(2,1)} %gather_fusion.3, bf16[10,688,1408]{2,1,0:T(8,128)(2,1)} %gather_fusion.2, bf16[10,688,1408]{2,1,0:T(8,128)(2,1)} %gather_fusion.1, pred[10]{0:T(512)(128)(4,1)S(1)} %compare_and_fusion), kind=kOutput, calls=%fused_computation.19 | convolution fusion | flops 7411466240 | bytes 70369288 | tf_op jit(solution)/shard_map/bkw,bfw->bkf/dot_general | solution.py:77
  501.4 8.1 %gather_fusion = f32[1024,688]{1,0:T(8,128)} fusion(f32[1280,688]{1,0:T(8,128)} %bitcast.30, s32[1024]{0:T(1024)S(1)} %copy-done.8), kind=kCustom, calls=%fused_computation | custom fusion | bytes 5640192 | tf_op jit(solution)/shard_map/gather | solution.py:79
  509.5 5.1 multiply_convert_fusion
  514.6 2.5 copy.32
  517.2 2.5 copy.33
  519.7 7.0 %reduce-scatter.5.cloned.1.call-done = bf16[3,688,512]{2,1,0:T(8,128)(2,1)} async-done(((bf16[3,688,1024]{2,1,0:T(8,128)(2,1)}), bf16[3,688,512]{2,1,0:T(8,128)(2,1)}) %reduce-scatter.5.cloned.1.call-update) | async-done | bytes 2113552 | tf_op jit(solution)/shard_map/reduce_scatter | solution.py:30
  526.7 4.2 convert_element_type.76
  (26 shorter events, 0.1 us)
Async XLA Ops:
  7.2 65.2 %copy-start.5 = (s32[1024]{0:T(1024)S(1)}, s32[1024]{0:T(1024)}, u32[]{:S(2)}) copy-start(s32[1024]{0:T(1024)} %param.11) | copy-start | bytes 12292
  7.2 76.3 %copy-start.4 = (bf16[1024,688]{0,1:T(8,128)(2,1)S(1)}, bf16[1024,688]{0,1:T(8,128)(2,1)}, u32[]{:S(2)}) copy-start(bf16[1024,688]{0,1:T(8,128)(2,1)} %param.13) | copy-start | bytes 4227076
  7.2 65.1 %all-gather.6.cloned.1.call-start = ((), (), s32[]{:S(2)}) async-start(), calls=%async_computation.6 | async-start | bytes 6340608 | tf_op jit(solution)/shard_map/all_gather | solution.py:24
  9.3 10.8 %all-to-all-start = ((f32[8,1,3]{2,1,0:T(1,128)}), f32[8,1,3]{2,1,0:T(1,128)S(1)}, u32[]{:S(2)}, u32[]{:S(2)}) async-start(f32[8,1,3]{2,1,0:T(1,128)} %broadcast_in_dim.15), calls=%async_computation | async-start | bytes 8192 | tf_op jit(solution)/shard_map/all_to_all | solution.py:13
  15.2 138.2 %all-gather.4.cloned.1.call-start = ((), (), s32[]{:S(2)}) async-start(), calls=%async_computation.3 | async-start | bytes 8912896 | tf_op jit(solution)/shard_map/all_gather | solution.py:47
  23.1 289.3 %all-gather.8.cloned.1.call-start = ((), (), s32[]{:S(2)}) async-start(), calls=%async_computation.7 | async-start | bytes 21135360 | tf_op jit(solution)/shard_map/all_gather | solution.py:24
  72.4 395.2 %reduce-scatter.3.cloned.1.call-start = ((), (), s32[]{:S(2)}) async-start(), calls=%async_computation.4 | async-start | bytes 21135360 | tf_op jit(solution)/shard_map/reduce_scatter | solution.py:30
  84.1 88.6 %copy-start = (bf16[1024,688]{1,0:T(8,128)(2,1)}, bf16[1024,688]{1,0:T(8,128)(2,1)S(1)}, u32[]{:S(2)}) copy-start(bf16[1024,688]{1,0:T(8,128)(2,1)S(1)} %copy.28) | copy-start | bytes 4227076
  86.4 86.4 %copy-start.2 = (bf16[1024,688]{1,0:T(8,128)(2,1)}, bf16[1024,688]{1,0:T(8,128)(2,1)S(1)}, u32[]{:S(2)}) copy-start(bf16[1024,688]{1,0:T(8,128)(2,1)S(1)} %copy.29) | copy-start | bytes 4227076
  87.4 85.4 %copy-start.6 = (s32[1024,1]{0,1:T(1,128)}, s32[1024,1]{0,1:T(1,128)S(1)}, u32[]{:S(2)}) copy-start(s32[1024,1]{0,1:T(1,128)S(1)} %compare_select_fusion) | copy-start | bytes 12292
  310.1 1.6 copy-start.7
  310.2 216.6 %reduce-scatter.5.cloned.1.call-start = ((), (), s32[]{:S(2)}) async-start(), calls=%async_computation.5 | async-start | bytes 6340608 | tf_op jit(solution)/shard_map/reduce_scatter | solution.py:30
  467.6 33.8 %copy-start.8 = (s32[1024]{0:T(1024)S(1)}, s32[1024]{0:T(1024)}, u32[]{:S(2)}) copy-start(s32[1024]{0:T(1024)} %broadcast_clamp_fusion) | copy-start | bytes 12292
  501.4 8.1 %copy-start.1 = (bf16[1024,688]{1,0:T(8,128)(2,1)S(1)}, bf16[1024,688]{1,0:T(8,128)(2,1)}, u32[]{:S(2)}) copy-start(bf16[1024,688]{1,0:T(8,128)(2,1)} %copy-done) | copy-start | bytes 4227076
  501.4 8.1 %copy-start.3 = (bf16[1024,688]{1,0:T(8,128)(2,1)S(1)}, bf16[1024,688]{1,0:T(8,128)(2,1)}, u32[]{:S(2)}) copy-start(bf16[1024,688]{1,0:T(8,128)(2,1)} %copy-done.2) | copy-start | bytes 4227076
Sparse Core Ops, SparseCore 0:
  9.6 62.6 all-gather.5
  75.2 78.1 all-gather.3
  155.1 153.0 all-gather.7
  310.6 156.9 reduce-scatter.2
  469.8 56.8 reduce-scatter.4
where the time goes:
time: 539 us; the launch traced here: 537 us
  waiting for transfers between devices  221 us (41%)
  matrix products  128 us (24%)
  local copies, waits for them, and re-layouts  108 us (20%)
  other arithmetic  50.4 us (9%)
  between operations  23 us (4%)
  starting transfers between devices  6.31 us (1%)
    reduce_scatter x2, waiting for transfers between devices, sum_by_axis(): shard = lax.psum_scatter(shard, axis, scatter_dimension=dim, tiled=True)  108 us
    dot_general x9, matrix products, add_block(): lax.dot_general(rows_hidden, rows_scaled, (((0,), (0,)), ((), ())), prefe...  94.5 us
    all_gather x1, waiting for transfers between devices, shards(): scaled = lax.all_gather(scaled_part, 'tensor', axis=1, tiled=True)  58.6 us
    gather x5, local copies, waits for them, and re-layouts, shards(): chosen = jnp.take(weight_piece, block_kind, axis=0)  54.7 us
    all_gather x2, waiting for transfers between devices, gather_axes(): shard = lax.all_gather(shard, axis, axis=dim, tiled=True)  49.2 us
    dot_general x1, matrix products, shards(): jnp.einsum('bkw,bfw->bkf', columns, chosen, preferred_element_type=jnp.fl...  33.8 us
    another operation x3, other arithmetic, shards(): partial_sum = jnp.stack([kind_product(kind_id) for kind_id in range(3)])  26 us
    scatter x1, local copies, waits for them, and re-layouts, shards(): jnp.zeros((capacity, width_all), jnp.bfloat16).at[slot_index].set(scaled)  19.3 us
  transfers between devices with their start and end apart: 6, of which 5 were waited for; matrix products, arithmetic and copies ran while one was open for 53% of the time, Pallas kernels for 0%

commit v1 on v0

--- a/solution.py
+++ b/solution.py
@@ -44,7 +44,9 @@
     factor = tok_rows * groups / (3.0 * counts)
     token_scale = jnp.sum(local_onehot * factor[None, :], axis=1)
     scaled_part = (out_grad.astype(jnp.float32) * token_scale[:, None]).astype(jnp.bfloat16)
-    scaled = lax.all_gather(scaled_part, "tensor", axis=1, tiled=True)
+    scaled = jnp.concatenate(
+        lax.all_to_all(jnp.stack([scaled_part] * lax.axis_size("tensor")), "tensor", 0, 0), axis=1
+    )
     gate_val = gate_pre.astype(jnp.float32)
     up_val = up_pre.astype(jnp.float32)
     sigmoid_g = jax.nn.sigmoid(gate_val)

time: 539 us -> 602 us (1.12)
  local copies, waits for them, and re-layouts: 108 us -> 136 us
  waiting for transfers between devices: 221 us -> 249 us
  starting transfers between devices: 6.31 us -> 13.4 us
    all_to_all x0 -> x1, waiting for transfers between devices: none -> 73.1 us  [shards(): lax.all_to_all(jnp.stack([scaled_part] * lax.axis_size('tensor')), 'tenso...]
    all_gather x1 -> x0, waiting for transfers between devices: 58.6 us -> none  [shards(): scaled = lax.all_gather(scaled_part, 'tensor', axis=1, tiled=True)]
    all_gather x2, waiting for transfers between devices: 49.2 us -> 64.4 us  [gather_axes(): shard = lax.all_gather(shard, axis, axis=dim, tiled=True)]
    all_to_all x0 -> x1, local copies, waits for them, and re-layouts: none -> 12.3 us  [shards(): lax.all_to_all(jnp.stack([scaled_part] * lax.axis_size('tensor')), 'tenso...]
    reshape x0 -> x1, local copies, waits for them, and re-layouts: none -> 11.3 us  [shards(): jnp.concatenate(lax.all_to_all(jnp.stack([scaled_part] * lax.axis_size('t...]
    all_to_all x0 -> x1, starting transfers between devices: none -> 9 us  [shards(): lax.all_to_all(jnp.stack([scaled_part] * lax.axis_size('tensor')), 'tenso...]
    another operation x3 -> x4, local copies, waits for them, and re-layouts: 16.8 us -> 22 us
  transfers between devices with their start and end apart: 6 -> 6, of which waited for: 5 -> 5; matrix products, arithmetic and copies ran while one was open for 53% -> 52% of each run, Pallas kernels for 0% -> 0%
where the time goes in v1:
time: 602 us; the launch traced here: 600 us
  waiting for transfers between devices  249 us (41%)
  local copies, waits for them, and re-layouts  136 us (23%)
  matrix products  128 us (21%)
  other arithmetic  49.7 us (8%)
  between operations  23.2 us (4%)
  starting transfers between devices  13.4 us (2%)
    reduce_scatter x2, waiting for transfers between devices, sum_by_axis(): shard = lax.psum_scatter(shard, axis, scatter_dimension=dim, tiled=True)  106 us
    dot_general x9, matrix products, add_block(): lax.dot_general(rows_hidden, rows_scaled, (((0,), (0,)), ((), ())), prefe...  94.3 us
    all_to_all x1, waiting for transfers between devices, shards(): lax.all_to_all(jnp.stack([scaled_part] * lax.axis_size('tensor')), 'tenso...  73.1 us
    all_gather x2, waiting for transfers between devices, gather_axes(): shard = lax.all_gather(shard, axis, axis=dim, tiled=True)  64.4 us
    gather x5, local copies, waits for them, and re-layouts, shards(): chosen = jnp.take(weight_piece, block_kind, axis=0)  54.1 us
    dot_general x1, matrix products, shards(): jnp.einsum('bkw,bfw->bkf', columns, chosen, preferred_element_type=jnp.fl...  33.8 us
    another operation x3, other arithmetic, shards(): partial_sum = jnp.stack([kind_product(kind_id) for kind_id in range(3)])  25.9 us
    scatter x1, local copies, waits for them, and re-layouts, shards(): jnp.zeros((capacity, width_all), jnp.bfloat16).at[slot_index].set(scaled)  18.7 us
  transfers between devices with their start and end apart: 6, of which 5 were waited for; matrix products, arithmetic and copies ran while one was open for 52% of the time, Pallas kernels for 0%

profile of v1, /device:TPU:1, one launch (start us, length us, event | category | flops | bytes accessed | tf_op | source)
XLA Modules:
  0.0 599.8 jit_solution(13562110322689542036)
XLA Ops:
  7.2 0.0 all-gather.3.cloned.1.call-start
  7.2 0.7 all-gather.3.cloned.1.call-update
  7.9 0.0 all-gather.5.cloned.1.call-start
  7.9 64.4 %all-gather.3.cloned.1.call-done = bf16[3,688,1024]{2,1,0:T(8,128)(2,1)} async-done(((bf16[3,688,512]{2,1,0:T(8,128)(2,1)}), bf16[3,688,1024]{2,1,0:T(8,128)(2,1)}) %all-gather.3.cloned.1.call-update) | async-done | bytes 4227088 | tf_op jit(solution)/shard_map/all_gather | solution.py:24
  72.3 0.0 all-gather.5.cloned.1.call-update
  72.3 0.8 convert_reduce_fusion
  73.1 0.6 broadcast_in_dim.15
  73.7 4.0 all-to-all-start
  77.7 5.0 all-to-all-done
  82.7 0.8 select_reduce_fusion
  83.5 1.3 multiply_convert_fusion.1
  84.8 5.2 stack.20
  90.0 9.0 %all-to-all-start.1 = ((bf16[16,1024,256]{2,1,0:T(8,128)(2,1)}), bf16[16,1024,256]{2,1,0:T(8,128)(2,1)}, u32[]{:S(2)}, u32[]{:S(2)}) async-start(bf16[16,1024,256]{2,1,0:T(8,128)(2,1)} %stack.20), calls=%async_computation.1 | async-start | bytes 16777216 | tf_op jit(solution)/shard_map/all_to_all | solution.py:48
  99.0 0.0 reduce-scatter.3.cloned.1.call-start
  99.0 0.1 fusion.30
  99.2 0.7 fusion.40
  109.1 0.9 reduce-window.6
  110.0 0.2 slice_reduce_fusion
  110.2 0.2 reduce-window.9
  110.4 0.7 copy.50
  111.1 2.2 copy.51
  113.4 0.8 pad_add_fusion
  114.1 0.1 add_bitcast_fusion
  114.2 0.1 fusion.32
  114.4 7.4 %scatter_custom_fusion = bf16[1280,688]{1,0:T(8,128)(2,1)} fusion(s32[1024]{0:T(1024)S(1)} %bitcast.38, bf16[1024,688]{1,0:T(8,128)(2,1)S(1)} %copy.51, bf16[1024,688]{1,0:T(8,128)(2,1)S(1)} %copy.50, f32[]{:T(128)} %constant.119.clone.1, bf16[]{:T(256)} %constant.116.clone.1), kind=kCustom, calls=%fused_computation.46 | custom fusion | flops 5636096 | bytes 4907014 | tf_op jit(solution)/shard_map/scatter | solution.py:73
  121.8 73.1 %all-to-all-done.1 = bf16[16,1024,256]{2,1,0:T(8,128)(2,1)} async-done(((bf16[16,1024,256]{2,1,0:T(8,128)(2,1)}), bf16[16,1024,256]{2,1,0:T(8,128)(2,1)}, u32[]{:S(2)}, u32[]{:S(2)}) %all-to-all-start.1) | async-done | bytes 8388640 | tf_op jit(solution)/shard_map/all_to_all | solution.py:48
  194.8 12.3 %copy.53 = bf16[16,1024,256]{1,2,0:T(8,128)(2,1)} copy(bf16[16,1024,256]{2,1,0:T(8,128)(2,1)} %all-to-all-done.1) | data formatting | bytes 16777216 | tf_op jit(solution)/shard_map/all_to_all | solution.py:48
  207.1 11.3 %copy.54 = bf16[1024,4096]{1,0:T(8,128)(2,1)} copy(bf16[1024,4096]{0,1:T(8,128)(2,1)} %bitcast.35) | data formatting | bytes 16777216 | tf_op jit(solution)/shard_map/reshape | solution.py:47
  218.4 18.7 %scatter_custom_fusion.1 = bf16[1280,4096]{1,0:T(8,128)(2,1)} fusion(s32[1024]{0:T(1024)S(1)} %bitcast.39, bf16[1024,4096]{1,0:T(8,128)(2,1)} %copy.54, bf16[]{:T(256)} %constant.116.clone.1), kind=kCustom, calls=%fused_computation.30 | custom fusion | bytes 10486272 | tf_op jit(solution)/shard_map/scatter | solution.py:72
  237.1 5.6 broadcast.150.clone.2
  242.8 31.5 %while.30 = (s32[]{:T(128)}, f32[688,4096]{1,0:T(8,128)}, s32[]{:T(128)}, bf16[1280,688]{1,0:T(8,128)(2,1)}, bf16[1280,4096]{1,0:T(8,128)(2,1)}, /*index=5*/s32[]{:T(128)}, s32[]{:T(128)}, s32[]{:T(128)}, s32[]{:T(128)}) while((s32[]{:T(128)}, f32[688,4096]{1,0:T(8,128)}, s32[]{:T(128)}, bf16[1280,688]{1,0:T(8,128)(2,1)}, ...), condition=%wide.region_11.12_spmd, body=%wide.region_10.11_spmd.sunk | while | flops 724238336 | bytes 23790732 | solution.py:104
  242.8 10.5 %convolution_add_fusion.6 = f32[688,4096]{1,0:T(8,128)} fusion(f32[688,4096]{1,0:T(8,128)} %get-tuple-element.315, bf16[1280,4096]{1,0:T(8,128)(2,1)} %get-tuple-element.327, s32[]{:T(128)S(6)} %select_n.91, bf16[1280,688]{1,0:T(8,128)(2,1)} %get-tuple-element.326), kind=kOutput, calls=%fused_computation.6.clone.1 | convolution fusion | flops 724238336 | bytes 23790592 | tf_op jit(solution)/shard_map/while/body/dot_general | solution.py:97
  253.3 10.5 %convolution_add_fusion.6 = f32[688,4096]{1,0:T(8,128)} fusion(f32[688,4096]{1,0:T(8,128)} %get-tuple-element.315, bf16[1280,4096]{1,0:T(8,128)(2,1)} %get-tuple-element.327, s32[]{:T(128)S(6)} %select_n.91, bf16[1280,688]{1,0:T(8,128)(2,1)} %get-tuple-element.326), kind=kOutput, calls=%fused_computation.6.clone.1 | convolution fusion | flops 724238336 | bytes 23790592 | tf_op jit(solution)/shard_map/while/body/dot_general | solution.py:97
  263.8 10.5 %convolution_add_fusion.6 = f32[688,4096]{1,0:T(8,128)} fusion(f32[688,4096]{1,0:T(8,128)} %get-tuple-element.315, bf16[1280,4096]{1,0:T(8,128)(2,1)} %get-tuple-element.327, s32[]{:T(128)S(6)} %select_n.91, bf16[1280,688]{1,0:T(8,128)(2,1)} %get-tuple-element.326), kind=kOutput, calls=%fused_computation.6.clone.1 | convolution fusion | flops 724238336 | bytes 23790592 | tf_op jit(solution)/shard_map/while/body/dot_general | solution.py:97
  274.3 7.6 %convert_bitcast_fusion.2 = bf16[1,688,4096]{2,1,0:T(8,128)(2,1)} fusion(f32[688,4096]{1,0:T(8,128)} %get-tuple-element.87), kind=kLoop, calls=%fused_computation.29 | loop fusion | flops 2818048 | bytes 16908288 | tf_op jit(solution)/shard_map/stack | solution.py:108
  281.8 5.5 broadcast.150.clone.1
  287.3 20.7 %while.31 = (s32[]{:T(128)}, f32[688,4096]{1,0:T(8,128)}, s32[]{:T(128)}, bf16[1280,688]{1,0:T(8,128)(2,1)}, bf16[1280,4096]{1,0:T(8,128)(2,1)}, /*index=5*/s32[]{:T(128)}, s32[]{:T(128)}, s32[]{:T(128)}, s32[]{:T(128)}) while((s32[]{:T(128)}, f32[688,4096]{1,0:T(8,128)}, s32[]{:T(128)}, bf16[1280,688]{1,0:T(8,128)(2,1)}, ...), condition=%wide.region_13.14_spmd, body=%wide.region_12.13_spmd.sunk | while | flops 724238336 | bytes 23790732 | solution.py:104
  287.3 10.4 %convolution_add_fusion.7 = f32[688,4096]{1,0:T(8,128)} fusion(f32[688,4096]{1,0:T(8,128)} %get-tuple-element.288, bf16[1280,4096]{1,0:T(8,128)(2,1)} %get-tuple-element.300, s32[]{:T(128)S(6)} %select_n.92, bf16[1280,688]{1,0:T(8,128)(2,1)} %get-tuple-element.299), kind=kOutput, calls=%fused_computation.10.clone.1 | convolution fusion | flops 724238336 | bytes 23790592 | tf_op jit(solution)/shard_map/while/body/dot_general | solution.py:97
  297.7 10.4 %convolution_add_fusion.7 = f32[688,4096]{1,0:T(8,128)} fusion(f32[688,4096]{1,0:T(8,128)} %get-tuple-element.288, bf16[1280,4096]{1,0:T(8,128)(2,1)} %get-tuple-element.300, s32[]{:T(128)S(6)} %select_n.92, bf16[1280,688]{1,0:T(8,128)(2,1)} %get-tuple-element.299), kind=kOutput, calls=%fused_computation.10.clone.1 | convolution fusion | flops 724238336 | bytes 23790592 | tf_op jit(solution)/shard_map/while/body/dot_general | solution.py:97
  308.1 5.6 broadcast.150.clone
  313.7 42.0 %while.32 = (s32[]{:T(128)}, f32[688,4096]{1,0:T(8,128)}, s32[]{:T(128)}, bf16[1280,688]{1,0:T(8,128)(2,1)}, bf16[1280,4096]{1,0:T(8,128)(2,1)}, /*index=5*/s32[]{:T(128)}, s32[]{:T(128)}, s32[]{:T(128)}, s32[]{:T(128)}) while((s32[]{:T(128)}, f32[688,4096]{1,0:T(8,128)}, s32[]{:T(128)}, bf16[1280,688]{1,0:T(8,128)(2,1)}, ...), condition=%wide.region_15.16_spmd, body=%wide.region_14.15_spmd.sunk | while | flops 724238336 | bytes 23790732 | solution.py:104
  313.7 10.5 %convolution_add_fusion.8 = f32[688,4096]{1,0:T(8,128)} fusion(f32[688,4096]{1,0:T(8,128)} %get-tuple-element.261, bf16[1280,4096]{1,0:T(8,128)(2,1)} %get-tuple-element.273, s32[]{:T(128)S(6)} %select_n.93, bf16[1280,688]{1,0:T(8,128)(2,1)} %get-tuple-element.272), kind=kOutput, calls=%fused_computation.14.clone.1 | convolution fusion | flops 724238336 | bytes 23790592 | tf_op jit(solution)/shard_map/while/body/dot_general | solution.py:97
  324.2 10.6 %convolution_add_fusion.8 = f32[688,4096]{1,0:T(8,128)} fusion(f32[688,4096]{1,0:T(8,128)} %get-tuple-element.261, bf16[1280,4096]{1,0:T(8,128)(2,1)} %get-tuple-element.273, s32[]{:T(128)S(6)} %select_n.93, bf16[1280,688]{1,0:T(8,128)(2,1)} %get-tuple-element.272), kind=kOutput, calls=%fused_computation.14.clone.1 | convolution fusion | flops 724238336 | bytes 23790592 | tf_op jit(solution)/shard_map/while/body/dot_general | solution.py:97
  334.8 10.5 %convolution_add_fusion.8 = f32[688,4096]{1,0:T(8,128)} fusion(f32[688,4096]{1,0:T(8,128)} %get-tuple-element.261, bf16[1280,4096]{1,0:T(8,128)(2,1)} %get-tuple-element.273, s32[]{:T(128)S(6)} %select_n.93, bf16[1280,688]{1,0:T(8,128)(2,1)} %get-tuple-element.272), kind=kOutput, calls=%fused_computation.14.clone.1 | convolution fusion | flops 724238336 | bytes 23790592 | tf_op jit(solution)/shard_map/while/body/dot_general | solution.py:97
  345.3 10.5 %convolution_add_fusion.8 = f32[688,4096]{1,0:T(8,128)} fusion(f32[688,4096]{1,0:T(8,128)} %get-tuple-element.261, bf16[1280,4096]{1,0:T(8,128)(2,1)} %get-tuple-element.273, s32[]{:T(128)S(6)} %select_n.93, bf16[1280,688]{1,0:T(8,128)(2,1)} %get-tuple-element.272), kind=kOutput, calls=%fused_computation.14.clone.1 | convolution fusion | flops 724238336 | bytes 23790592 | tf_op jit(solution)/shard_map/while/body/dot_general | solution.py:97
  355.8 8.3 %convert_bitcast_fusion = (bf16[1,688,4096]{2,1,0:T(8,128)(2,1)S(1)}, bf16[1,688,4096]{2,1,0:T(8,128)(2,1)S(1)}) fusion(f32[688,4096]{1,0:T(8,128)} %get-tuple-element.89, f32[688,4096]{1,0:T(8,128)} %get-tuple-element.88), kind=kLoop, calls=%fused_computation.27 | loop fusion | flops 5636096 | bytes 33816576 | tf_op jit(solution)/shard_map/stack | solution.py:108
  364.1 10.1 %pad_maximum_fusion = bf16[3,688,4096]{2,1,0:T(8,128)(2,1)} fusion(bf16[1,688,4096]{2,1,0:T(8,128)(2,1)S(1)} %get-tuple-element.153, bf16[1,688,4096]{2,1,0:T(8,128)(2,1)S(1)} %get-tuple-element.154, bf16[1,688,4096]{2,1,0:T(8,128)(2,1)} %convert_bitcast_fusion.2), kind=kLoop, calls=%fused_computation.26 | loop fusion | flops 16908288 | bytes 33816576 | tf_op jit(solution)/shard_map/stack | solution.py:108
  374.2 0.3 reduce-scatter.5.cloned.1.call-start
  374.5 0.7 fusion.35
  375.2 0.7 compare_and_fusion
  375.9 0.6 broadcast_clamp_fusion
  376.5 9.8 %fusion.39 = (bf16[3,688,1408]{2,1,0:T(8,128)(2,1)}, bf16[3,688,1408]{2,1,0:T(8,128)(2,1)}) fusion(bf16[3,688,4096]{2,1,0:T(8,128)(2,1)} %all-gather.5.cloned.1.call-done), kind=kLoop, calls=%fused_computation.85 | loop fusion | bytes 23248896 | tf_op jit(solution)/shard_map/jit(_take)/gather | solution.py:78
  386.2 14.1 %gather_fusion.1 = bf16[10,688,1408]{2,1,0:T(8,128)(2,1)} fusion(bf16[3,688,1408]{2,1,0:T(8,128)(2,1)} %get-tuple-element.146, s32[1024]{0:T(1024)S(1)} %pad_clamp_fusion), kind=kCustom, calls=%fused_computation.1 | custom fusion | bytes 38748200 | tf_op jit(solution)/shard_map/jit(_take)/gather | solution.py:78
  400.3 14.3 %gather_fusion.2 = bf16[10,688,1408]{2,1,0:T(8,128)(2,1)} fusion(bf16[3,688,1408]{2,1,0:T(8,128)(2,1)} %get-tuple-element.147, s32[1024]{0:T(1024)S(1)} %pad_clamp_fusion), kind=kCustom, calls=%fused_computation.2 | custom fusion | bytes 38748200 | tf_op jit(solution)/shard_map/jit(_take)/gather | solution.py:78
  414.6 5.2 mini-gather-slice.5
  419.8 10.7 %gather_fusion.3 = bf16[10,688,1280]{2,1,0:T(8,128)(2,1)} fusion(bf16[3,688,1280]{2,1,0:T(8,128)(2,1)} %mini-gather-slice.5, s32[1024]{0:T(1024)S(1)} %pad_clamp_fusion), kind=kCustom, calls=%fused_computation.3 | custom fusion | bytes 35225640 | tf_op jit(solution)/shard_map/jit(_take)/gather | solution.py:78
  430.5 99.3 %reduce-scatter.3.cloned.1.call-done = bf16[3,688,1024]{2,1,0:T(8,128)(2,1)} async-done(((bf16[3,688,4096]{2,1,0:T(8,128)(2,1)}), bf16[3,688,1024]{2,1,0:T(8,128)(2,1)}) %reduce-scatter.3.cloned.1.call-update) | async-done | bytes 4227088 | tf_op jit(solution)/shard_map/reduce_scatter | solution.py:30
  529.9 33.8 %fusion.9 = f32[10,128,688]{2,1,0:T(8,128)} fusion(bf16[10,128,4096]{2,1,0:T(8,128)(2,1)} %bitcast.34, bf16[10,688,1280]{2,1,0:T(8,128)(2,1)} %gather_fusion.3, bf16[10,688,1408]{2,1,0:T(8,128)(2,1)} %gather_fusion.2, bf16[10,688,1408]{2,1,0:T(8,128)(2,1)} %gather_fusion.1, pred[10]{0:T(512)(128)(4,1)S(1)} %compare_and_fusion), kind=kOutput, calls=%fused_computation.19 | convolution fusion | flops 7411466240 | bytes 70369288 | tf_op jit(solution)/shard_map/bkw,bfw->bkf/dot_general | solution.py:79
  563.7 8.1 %gather_fusion = f32[1024,688]{1,0:T(8,128)} fusion(f32[1280,688]{1,0:T(8,128)} %bitcast.33, s32[1024]{0:T(1024)S(1)} %copy-done.8), kind=kCustom, calls=%fused_computation | custom fusion | bytes 5640192 | tf_op jit(solution)/shard_map/gather | solution.py:81
  571.8 5.1 multiply_convert_fusion
  576.9 2.5 copy.56
  579.5 2.5 copy.57
  582.0 7.1 %reduce-scatter.5.cloned.1.call-done = bf16[3,688,512]{2,1,0:T(8,128)(2,1)} async-done(((bf16[3,688,1024]{2,1,0:T(8,128)(2,1)}), bf16[3,688,512]{2,1,0:T(8,128)(2,1)}) %reduce-scatter.5.cloned.1.call-update) | async-done | bytes 2113552 | tf_op jit(solution)/shard_map/reduce_scatter | solution.py:30
  589.0 4.2 convert_element_type.76
  (28 shorter events, 0.1 us)
Async XLA Ops:
  7.2 65.1 %all-gather.3.cloned.1.call-start = ((), (), s32[]{:S(2)}) async-start(), calls=%async_computation.6 | async-start | bytes 6340608 | tf_op jit(solution)/shard_map/all_gather | solution.py:24
  7.9 368.6 %all-gather.5.cloned.1.call-start = ((), (), s32[]{:S(2)}) async-start(), calls=%async_computation.7 | async-start | bytes 21135360 | tf_op jit(solution)/shard_map/all_gather | solution.py:24
  73.7 8.9 %all-to-all-start = ((f32[8,1,3]{2,1,0:T(1,128)}), f32[8,1,3]{2,1,0:T(1,128)S(1)}, u32[]{:S(2)}, u32[]{:S(2)}) async-start(f32[8,1,3]{2,1,0:T(1,128)} %broadcast_in_dim.15), calls=%async_computation | async-start | bytes 8192 | tf_op jit(solution)/shard_map/all_to_all | solution.py:13
  90.0 9.0 %copy-start.5 = (s32[1024]{0:T(1024)S(1)}, s32[1024]{0:T(1024)}, u32[]{:S(2)}) copy-start(s32[1024]{0:T(1024)} %param.11) | copy-start | bytes 12292
  90.0 20.4 %copy-start.4 = (bf16[1024,688]{0,1:T(8,128)(2,1)S(1)}, bf16[1024,688]{0,1:T(8,128)(2,1)}, u32[]{:S(2)}) copy-start(bf16[1024,688]{0,1:T(8,128)(2,1)} %param.13) | copy-start | bytes 4227076
  90.0 104.9 %all-to-all-start.1 = ((bf16[16,1024,256]{2,1,0:T(8,128)(2,1)}), bf16[16,1024,256]{2,1,0:T(8,128)(2,1)}, u32[]{:S(2)}, u32[]{:S(2)}) async-start(bf16[16,1024,256]{2,1,0:T(8,128)(2,1)} %stack.20), calls=%async_computation.1 | async-start | bytes 16777216 | tf_op jit(solution)/shard_map/all_to_all | solution.py:48
  99.0 430.8 %reduce-scatter.3.cloned.1.call-start = ((), (), s32[]{:S(2)}) async-start(), calls=%async_computation.4 | async-start | bytes 21135360 | tf_op jit(solution)/shard_map/reduce_scatter | solution.py:30
  111.1 96.1 %copy-start = (bf16[1024,688]{1,0:T(8,128)(2,1)}, bf16[1024,688]{1,0:T(8,128)(2,1)S(1)}, u32[]{:S(2)}) copy-start(bf16[1024,688]{1,0:T(8,128)(2,1)S(1)} %copy.50) | copy-start | bytes 4227076
  113.3 93.8 %copy-start.2 = (bf16[1024,688]{1,0:T(8,128)(2,1)}, bf16[1024,688]{1,0:T(8,128)(2,1)S(1)}, u32[]{:S(2)}) copy-start(bf16[1024,688]{1,0:T(8,128)(2,1)S(1)} %copy.51) | copy-start | bytes 4227076
  114.3 104.0 %copy-start.6 = (s32[1024,1]{0,1:T(1,128)}, s32[1024,1]{0,1:T(1,128)S(1)}, u32[]{:S(2)}) copy-start(s32[1024,1]{0,1:T(1,128)S(1)} %compare_select_fusion) | copy-start | bytes 12292
  374.1 1.7 copy-start.7
  374.2 214.9 %reduce-scatter.5.cloned.1.call-start = ((), (), s32[]{:S(2)}) async-start(), calls=%async_computation.5 | async-start | bytes 6340608 | tf_op jit(solution)/shard_map/reduce_scatter | solution.py:30
  529.9 33.8 %copy-start.8 = (s32[1024]{0:T(1024)S(1)}, s32[1024]{0:T(1024)}, u32[]{:S(2)}) copy-start(s32[1024]{0:T(1024)} %broadcast_clamp_fusion) | copy-start | bytes 12292
  563.7 8.1 %copy-start.1 = (bf16[1024,688]{1,0:T(8,128)(2,1)S(1)}, bf16[1024,688]{1,0:T(8,128)(2,1)}, u32[]{:S(2)}) copy-start(bf16[1024,688]{1,0:T(8,128)(2,1)} %copy-done) | copy-start | bytes 4227076
  563.7 8.1 %copy-start.3 = (bf16[1024,688]{1,0:T(8,128)(2,1)S(1)}, bf16[1024,688]{1,0:T(8,128)(2,1)}, u32[]{:S(2)}) copy-start(bf16[1024,688]{1,0:T(8,128)(2,1)} %copy-done.2) | copy-start | bytes 4227076
Sparse Core Ops, SparseCore 0:
  9.6 62.6 all-gather.2
  74.0 157.2 all-gather.4
  374.3 155.5 reduce-scatter.2
  532.1 56.9 reduce-scatter.4
